TPU v7x, 256 devices: a whole 4x4x8 slice. The times are simulated.
256 devices in a mesh: section: 16 (over y, z_lo, core), dp: 4 (over x), mp: 4 (over z_hi).
Axes of the slice: x: 4, y: 4, z: 8 (z_hi: 4, z_lo: 2; z = z_hi * 2 + z_lo), core: 2. Of those that a mesh axis runs over, the one named last changes fastest.
Arguments:
- patches: bfloat16 [32768, 1280], P(('section', 'dp')), may hold values from -6 to 6
- patch_counts: int32 [128], P(('section', 'dp')), may hold values from 8 to 256, as said below
- dest_rows: int32 [8192], P(('section', 'dp')), may hold values from 0 to 32767, as said below
- qkv_weight: bfloat16 [1280, 3, 1280], P(None, None, 'mp'), may hold values from -1 to 1
- out_weight: bfloat16 [1280, 1280], P('mp'), may hold values from -0.15625 to 0.15625
- attn_gain: bfloat16 [1280], replicated, may hold values from 0.25 to 1.75
- merge_gain: bfloat16 [1280], replicated, may hold values from 0.25 to 1.75
- fc1_weight: bfloat16 [5120, 5120], P('mp', ('section', 'dp')), may hold values from -0.078125 to 0.078125
- fc1_bias: bfloat16 [5120], P(('section', 'dp')), may hold values from -3 to 3
- fc2_weight: bfloat16 [5120, 8192], P(('section', 'dp'), 'mp'), may hold values from -0.078125 to 0.078125
- fc2_bias: bfloat16 [8192], P('mp'), may hold values from -3 to 3
- text_embeds: bfloat16 [32768, 8192], P(('section', 'dp'), 'mp'), may hold values from -6 to 6
- section_hidden: bfloat16 [32768, 8192], P(('section', 'dp'), 'mp'), may hold values from -80 to 80
- llm_gain: bfloat16 [8192], P('mp'), may hold values from 0.25 to 1.75
Outputs:
- sequence_embeds: bfloat16 [32768, 8192], P(('section', 'dp'), 'mp')
- layer_inputs: bfloat16 [32768, 8192], P(('section', 'dp'), 'mp')
Inputs may be any that keep to these rules, and one draw needn't show every extreme that they name: `patch_counts`: multiples of 4; a tile's patches fill the first slots of its block. `dest_rows`: all rows differ. Each group's merged slots form runs of 2 consecutive slots (aligned); a run goes to one sequence slice (row // 512, numbered in section-major order), different runs of a group to different slices. Rows of slots that are not live are never written.
All inputs are finite; a program needn't handle non-finite values.
Results may differ from a plain program's by a relative error of at most 0.0055.
Values may be sent and summed in bfloat16 or wider, within the bound.
A program may use at most 128 MiB of HBM per device.

v0:
```python
import jax
import jax.numpy as jnp
from jax import lax
from jax.sharding import PartitionSpec as P

HEAD_DIM = 80
HID = 8192
vit_eps = 1e-06
llm_eps = 1e-06


def gather_turned(arrays, axis, dims):
    turned = [jnp.moveaxis(a, dim, 0) for a, dim in zip(arrays, dims)]
    widths = [t[0].size for t in turned]
    both = jnp.concatenate([t.reshape(-1, w) for t, w in zip(turned, widths)], axis=1)
    out = lax.all_gather(both, axis, axis=0, tiled=True)
    blocks = jnp.split(out, [sum(widths[:k]) for k in range(1, len(widths))], axis=1)
    return tuple(
        (
            jnp.moveaxis(b.reshape(-1, *t.shape[1:]), 0, dim)
            for b, t, dim in zip(blocks, turned, dims)
        )
    )


def joined_along(blocks, dim):
    blocks = jnp.moveaxis(blocks, 0, dim)
    shape = blocks.shape
    return blocks.reshape(*shape[:dim], shape[dim] * shape[dim + 1], *shape[dim + 2 :])


def copy_for_each(value, axis):
    copies = jnp.broadcast_to(value, (lax.axis_size(axis), *value.shape))
    return lax.all_to_all(copies, axis, split_axis=0, concat_axis=0, tiled=True)


def gathered_copies(value, axis, dim):
    return joined_along(copy_for_each(value, axis), dim)


def cut_along(value, dim, devices):
    before, after = (value.shape[:dim], value.shape[dim + 1 :])
    return jnp.moveaxis(value.reshape(*before, devices, -1, *after), dim, 0)


def sent_and_summed(value, axis, dim):
    devices = lax.axis_size(axis)
    blocks = lax.all_to_all(cut_along(value, dim, devices), axis, 0, 0, tiled=True)
    return jnp.sum(blocks.astype(jnp.float32), axis=0)


def from_behind(value, axis, steps):
    count = lax.axis_size(axis)
    first, last = (max(0, -steps), min(count, count - steps))
    return lax.ppermute(value, axis, [(source, source + steps) for source in range(first, last)])


def over_copies(value, axis):
    return copy_for_each(value, axis).sum(axis=0)


def layer_norm(values, gain):
    centred = values.astype(jnp.float32)
    centred = centred - jnp.mean(centred, axis=-1, keepdims=True)
    variance = jnp.mean(centred * centred, axis=-1, keepdims=True)
    return centred * lax.rsqrt(variance + vit_eps) * gain.astype(jnp.float32)


def per_device(
    patches,
    patch_counts,
    dest_rows,
    qkv_weight,
    out_weight,
    attn_gain,
    merge_gain,
    fc1_weight,
    fc1_bias,
    fc2_weight,
    fc2_bias,
    text_embeds,
    section_hidden,
    llm_gain,
):
    width = patches.shape[1]
    tile_total = patch_counts.shape[0]
    block_rows = patches.shape[0] // tile_total
    merged_rows = patches.shape[0] // 4
    local_cols = qkv_weight.shape[2]
    local_heads = local_cols // HEAD_DIM
    feature_cols = text_embeds.shape[1]
    seq_rows = text_embeds.shape[0]
    section_count = lax.axis_size("section")
    group_count = section_count * lax.axis_size("dp")
    run_cap = max(2, merged_rows // group_count)
    run_total = merged_rows // run_cap
    normed_in = layer_norm(patches, attn_gain).astype(jnp.bfloat16)
    projections = jnp.dot(
        normed_in, qkv_weight.reshape(width, 3 * local_cols), preferred_element_type=jnp.float32
    ).astype(jnp.bfloat16)
    projections = projections.reshape(tile_total, block_rows, 3, local_heads, HEAD_DIM)
    query_part = projections[:, :, 0]
    key_part = projections[:, :, 1]
    value_part = projections[:, :, 2]
    scores = jnp.einsum(
        "tqhd,tkhd->thqk", query_part, key_part, preferred_element_type=jnp.float32
    ) * HEAD_DIM ** (-0.5)
    key_live = (
        jnp.arange(block_rows, dtype=jnp.int32)[None, None, None, :]
        < patch_counts[:, None, None, None]
    )
    scores = jnp.where(key_live, scores, -1e30)
    weights = jax.nn.softmax(scores, axis=-1).astype(jnp.bfloat16)
    attended = jnp.einsum(
        "thqk,tkhd->tqhd", weights, value_part, preferred_element_type=jnp.float32
    ).astype(jnp.bfloat16)
    attended = attended.reshape(patches.shape[0], local_cols)
    partial_proj = jnp.dot(attended, out_weight, preferred_element_type=jnp.float32)
    position = lax.axis_index("mp")
    own_patch = lax.dynamic_slice_in_dim(
        patches.reshape(merged_rows, 4, width), position, 1, 1
    ).reshape(merged_rows, width)
    own_proj = lax.psum_scatter(
        partial_proj.reshape(merged_rows, 4, width), "mp", scatter_dimension=1, tiled=True
    ).reshape(merged_rows, width)
    block_out = (own_patch.astype(jnp.float32) + own_proj).astype(jnp.bfloat16)
    merge_part = layer_norm(block_out, merge_gain).astype(jnp.bfloat16)
    first_full, second_full, bias_full = gather_turned(
        (fc1_weight, fc2_weight, fc1_bias), "section", (1, 0, 0)
    )
    first_partial = jnp.dot(
        gathered_copies(merge_part, "dp", 0), first_full, preferred_element_type=jnp.float32
    )
    first_total = lax.psum(first_partial.astype(jnp.bfloat16), "mp").astype(jnp.float32)
    hidden = jax.nn.gelu(first_total + bias_full.astype(jnp.float32), approximate=False).astype(
        jnp.bfloat16
    )
    embed_total = sent_and_summed(
        jnp.dot(hidden, second_full, preferred_element_type=jnp.float32).astype(jnp.bfloat16),
        "dp",
        0,
    )
    image_embeds = (embed_total + fc2_bias.astype(jnp.float32)).astype(jnp.bfloat16)
    slot_in_tile = jnp.arange(merged_rows, dtype=jnp.int32) % (block_rows // 4)
    tile_counts = jnp.repeat(patch_counts, block_rows // 4, total_repeat_length=merged_rows)
    live = slot_in_tile * 4 < tile_counts
    receiver = dest_rows // seq_rows
    run_target = receiver.reshape(run_total, run_cap)[:, 0]
    place = jnp.where(live, dest_rows % seq_rows, seq_rows)
    send_rows = (
        jnp.zeros((group_count, run_cap, feature_cols), jnp.bfloat16)
        .at[run_target]
        .set(image_embeds.reshape(run_total, run_cap, feature_cols))
    )
    send_place = (
        jnp.full((group_count, run_cap), seq_rows, jnp.int32)
        .at[run_target]
        .set(place.reshape(run_total, run_cap))
    )
    got_rows, got_place = (
        lax.all_to_all(send_rows, ("section", "dp"), split_axis=0, concat_axis=0, tiled=True),
        lax.all_to_all(send_place, ("section", "dp"), split_axis=0, concat_axis=0, tiled=True),
    )
    sequence_embeds = text_embeds.at[got_place.reshape(-1)].set(
        got_rows.reshape(-1, feature_cols), mode="drop"
    )
    incoming = from_behind(section_hidden, "section", 1)
    entering = jnp.where(lax.axis_index("section") == 0, sequence_embeds, incoming).astype(
        jnp.float32
    )
    row_total = over_copies(jnp.sum(entering * entering, axis=1), "mp")
    layer_inputs = (
        entering * lax.rsqrt(row_total / HID + llm_eps)[:, None] * llm_gain.astype(jnp.float32)
    ).astype(jnp.bfloat16)
    return (sequence_embeds, layer_inputs)


def solution(mesh):
    in_specs = (
        P(("section", "dp"), None),
        P(("section", "dp")),
        P(("section", "dp")),
        P(None, None, "mp"),
        P("mp", None),
        P(),
        P(),
        P("mp", ("section", "dp")),
        P(("section", "dp")),
        P(("section", "dp"), "mp"),
        P("mp"),
        P(("section", "dp"), "mp"),
        P(("section", "dp"), "mp"),
        P("mp"),
    )
    out_specs = (P(("section", "dp"), "mp"), P(("section", "dp"), "mp"))
    return jax.shard_map(
        per_device, mesh=mesh, in_specs=in_specs, out_specs=out_specs, check_vma=False
    )
```

profile of v0, /device:TPU:2, one launch (start us, length us, event | category | flops | bytes accessed | tf_op | source)
XLA Modules:
  0.0 325.1 jit_solution(17238749150550705226)
XLA Ops:
  8.0 0.0 copy-start
  8.0 0.0 reduce-scatter.2.cloned.1.call-start
  8.1 3.3 %copy.101 = bf16[512,2048]{1,0:T(8,128)(2,1)} copy(bf16[512,2048]{1,0:T(8,128)(2,1)} %param.27) | data formatting | bytes 4194304
  11.4 0.2 convert_reduce_fusion.1
  11.7 0.5 fusion.16
  12.2 2.6 convolution_convert_fusion
  14.8 2.5 reshape.190
  17.3 1.6 fusion.120
  18.9 0.1 iota_compare_fusion
  18.9 3.3 %fusion.122 = (f32[2,4,256]{2,1,0:T(4,128)S(1)}, f32[2,4,256,256]{2,3,1,0:T(8,128)}) fusion(pred[2,256]{1,0:T(4,128)(4,1)S(1)} %iota_compare_fusion, bf16[2,256,1,4,80]{1,0,4,3,2:T(2,128)(2,1)} %get-tuple-element.18, bf16[2,256,1,4,80]{1,0,4,3,2:T(2,128)(2,1)} %get-tuple-element.17), kind=kOutput, calls=%fused_computation.164 | convolution fusion | flops 85983488 | bytes 2761216 | tf_op jit(solution)/shard_map/sub | solution.py:113
  22.2 1.9 fusion.69
  24.1 0.3 copy.59
  24.4 0.5 dot_general.23
  24.9 0.0 copy-start.12
  25.0 0.0 copy-start.2
  25.0 3.6 %fusion.73 = f32[128,4,1280]{2,0,1:T(8,128)} fusion(bf16[320,1280]{1,0:T(8,128)(2,1)} %param.20, bf16[128,4,320]{2,1,0:T(4,128)(2,1)S(1)} %dot_general.23), kind=kOutput, calls=%fused_computation.91 | convolution fusion | flops 419430400 | bytes 3768320 | tf_op jit(solution)/shard_map/dot_general | solution.py:118
  28.6 0.0 reduce-scatter.2.cloned.1.call-update
  28.6 0.0 all-gather.2.cloned.1.call-start
  28.7 0.1 copy.61
  28.8 0.7 copy-done.4
  29.5 0.8 pad_maximum_fusion
  30.3 0.0 all-gather.2.cloned.1.call-update
  30.4 0.0 all-reduce.2.cloned.1.call-start
  30.4 3.5 %reshape.188 = bf16[128,4,1280]{2,1,0:T(4,128)(2,1)} reshape(bf16[512,1280]{1,0:T(8,128)(2,1)} %param.16) | data formatting | bytes 2621440 | tf_op jit(solution)/shard_map/reshape | solution.py:121
  33.9 2.0 constant_dynamic-slice_fusion
  35.9 69.9 %reduce-scatter.2.cloned.1.call-done = f32[128,1,1280]{2,0,1:T(8,128)} async-done(((f32[128,4,1280]{2,0,1:T(8,128)}), f32[128,1,1280]{2,0,1:T(8,128)}) %reduce-scatter.2.cloned.1.call-update) | async-done | bytes 655376 | tf_op jit(solution)/shard_map/reduce_scatter | solution.py:123
  105.9 1.3 convert_reduce_fusion.2
  107.1 0.2 fusion.78
  107.4 0.2 fusion.80
  107.6 0.1 broadcast_in_dim.30
  107.7 19.0 %all_to_all.30 = bf16[4,128,1280]{2,1,0:T(8,128)(2,1)} all-to-all(bf16[4,128,1280]{2,1,0:T(8,128)(2,1)S(1)} %broadcast_in_dim.30), channel_id=1, replica_groups=mesh['section'=16,'dp'=4,'mp'=4] {'dp'}, dimensions={0} | all-to-all | bytes 2621440 | tf_op jit(solution)/shard_map/all_to_all | solution.py:34
  126.7 3.4 %all-gather.2.cloned.1.call-done = bf16[1280,3329]{1,0:T(8,128)(2,1)} async-done(((bf16[80,3329]{1,0:T(8,128)(2,1)}), bf16[1280,3329]{1,0:T(8,128)(2,1)}) %all-gather.2.cloned.1.call-update) | async-done | bytes 8522256 | tf_op jit(solution)/shard_map/all_gather | solution.py:16
  130.1 5.3 %fusion.10 = bf16[512,1280]{1,0:T(8,128)(2,1)} fusion(bf16[512,1280]{1,0:T(8,128)(2,1)} %bitcast.62, bf16[1280,3329]{1,0:T(8,128)(2,1)} %all-gather.2.cloned.1.call-done), kind=kOutput, calls=%fused_computation.19 | convolution fusion | flops 1678376960 | bytes 5898240 | tf_op jit(solution)/shard_map/dot_general | solution.py:131
  135.4 0.0 all-reduce.2.cloned.1.call-update
  135.4 1.2 convert_reduce_fusion.3
  136.6 73.0 %all-reduce.2.cloned.1.call-done = bf16[512,1280]{1,0:T(8,128)(2,1)} async-done(((bf16[512,1280]{1,0:T(8,128)(2,1)}), bf16[512,1280]{1,0:T(8,128)(2,1)}) %all-reduce.2.cloned.1.call-update) | async-done | bytes 1310736 | tf_op jit(solution)/shard_map/psum | solution.py:134
  209.6 12.3 %fusion.13 = bf16[512,2048]{1,0:T(8,128)(2,1)} fusion(bf16[1280,3329]{1,0:T(8,128)(2,1)} %all-gather.2.cloned.1.call-done, bf16[512,1280]{1,0:T(8,128)(2,1)} %all-reduce.2.cloned.1.call-done, f32[1280]{0:T(1024)S(1)} %convert_reduce_fusion.3), kind=kOutput, calls=%fused_computation.20 | convolution fusion | flops 2729312256 | bytes 8655872 | tf_op jit(solution)/shard_map/dot_general | solution.py:139
  221.9 5.1 %all-to-all-start.2 = ((bf16[4,128,2048]{2,1,0:T(8,128)(2,1)}), bf16[4,128,2048]{2,1,0:T(8,128)(2,1)}, u32[]{:S(2)}, u32[]{:S(2)}) async-start(bf16[4,128,2048]{2,1,0:T(8,128)(2,1)} %bitcast.61), calls=%async_computation.3 | async-start | bytes 4194304 | tf_op jit(solution)/shard_map/all_to_all | solution.py:48
  227.1 2.9 collective-permute-start
  229.9 0.6 fusion.121
  230.5 1.2 compare_select_fusion.2
  231.8 0.1 reshape.185
  231.9 0.1 reshape.209
  232.1 0.1 fusion.83
  232.2 1.3 scatter_custom_fusion
  233.5 18.9 %all-to-all-done.2 = bf16[4,128,2048]{2,1,0:T(8,128)(2,1)} async-done(((bf16[4,128,2048]{2,1,0:T(8,128)(2,1)}), bf16[4,128,2048]{2,1,0:T(8,128)(2,1)}, u32[]{:S(2)}, u32[]{:S(2)}) %all-to-all-start.2) | async-done | bytes 2097184 | tf_op jit(solution)/shard_map/all_to_all | solution.py:48
  252.4 6.9 %all-to-all-start = ((s32[64,1,2]{2,1,0:T(1,128)}), s32[64,1,2]{2,1,0:T(1,128)S(1)}, u32[]{:S(2)}, u32[]{:S(2)}) async-start(s32[64,1,2]{2,1,0:T(1,128)} %bitcast.15), calls=%async_computation | async-start | bytes 65536 | tf_op jit(solution)/shard_map/all_to_all | solution.py:162
  259.3 2.1 convert_reduce_fusion
  261.3 1.6 reduce_sum.80
  262.9 1.6 add_convert_fusion
  264.6 1.1 broadcast_in_dim.24
  265.6 8.0 %scatter_fusion = bf16[64,2,2048]{2,1,0:T(2,128)(2,1)} fusion(bf16[64,2,2048]{2,1,0:T(2,128)(2,1)} %broadcast_in_dim.24, s32[64]{0:T(128)S(1)} %fusion.83, bf16[64,2,2048]{2,1,0:T(2,128)(2,1)S(1)} %add_convert_fusion), kind=kCustom, calls=%fused_computation.1 | custom fusion | bytes 1573120 | tf_op jit(solution)/shard_map/scatter | solution.py:153
  273.6 8.8 %all-to-all-start.3 = ((bf16[64,2,2048]{2,1,0:T(2,128)(2,1)}), bf16[64,2,2048]{2,1,0:T(2,128)(2,1)S(1)}, u32[]{:S(2)}, u32[]{:S(2)}) async-start(bf16[64,2,2048]{2,1,0:T(2,128)(2,1)} %scatter_fusion), calls=%async_computation.4 | async-start | bytes 1048576 | tf_op jit(solution)/shard_map/all_to_all | solution.py:161
  282.5 0.5 broadcast.203
  283.0 0.7 reduce.11
  283.7 0.1 reshape.187
  283.8 10.3 %all-to-all-done.3 = bf16[64,2,2048]{2,1,0:T(2,128)(2,1)S(1)} async-done(((bf16[64,2,2048]{2,1,0:T(2,128)(2,1)}), bf16[64,2,2048]{2,1,0:T(2,128)(2,1)S(1)}, u32[]{:S(2)}, u32[]{:S(2)}) %all-to-all-start.3) | async-done | bytes 524320 | tf_op jit(solution)/shard_map/all_to_all | solution.py:161
  294.1 0.2 reshape.225
  294.3 4.6 %scatter_fusion.1 = bf16[512,2048]{1,0:T(8,128)(2,1)} fusion(bf16[512,2048]{1,0:T(8,128)(2,1)} %copy.101, s32[128]{0:T(128)S(1)} %fusion.87, bf16[128,2048]{1,0:T(8,128)(2,1)S(1)} %reshape.225), kind=kCustom, calls=%fused_computation.2 | custom fusion | bytes 1573376 | tf_op jit(solution)/shard_map/scatter | solution.py:164
  298.9 2.4 fusion.3
  301.3 0.6 broadcast_in_dim.31
  301.9 3.9 %all-to-all-start.4 = ((f32[4,1,512]{2,1,0:T(1,128)}), f32[4,1,512]{2,1,0:T(1,128)S(1)}, u32[]{:S(2)}, u32[]{:S(2)}) async-start(f32[4,1,512]{2,1,0:T(1,128)} %broadcast_in_dim.31), calls=%async_computation.5 | async-start | bytes 16384 | tf_op jit(solution)/shard_map/all_to_all | solution.py:34
  305.8 7.7 %all-to-all-done.4 = f32[4,1,512]{2,1,0:T(1,128)S(1)} async-done(((f32[4,1,512]{2,1,0:T(1,128)}), f32[4,1,512]{2,1,0:T(1,128)S(1)}, u32[]{:S(2)}, u32[]{:S(2)}) %all-to-all-start.4) | async-done | bytes 8224 | tf_op jit(solution)/shard_map/all_to_all | solution.py:34
  313.5 4.1 %fusion.5 = bf16[512,2048]{1,0:T(8,128)(2,1)} fusion(f32[2048]{0:T(1024)S(1)} %convert_element_type.105, f32[512]{0:T(512)S(1)} %add_rsqrt_fusion, bf16[512,2048]{1,0:T(8,128)(2,1)} %scatter_fusion.1, bf16[512,2048]{1,0:T(8,128)(2,1)} %collective-permute-done, pred[]{:T(512)S(6)} %eq.6), kind=kLoop, calls=%fused_computation.10 | loop fusion | flops 5242880 | bytes 6301697 | tf_op jit(solution)/shard_map/convert_element_type | solution.py:174
  (35 shorter events, 0.1 us)
Async XLA Ops:
  8.0 4.2 %copy-start = (bf16[1280,3,320]{0,2,1:T(8,128)(2,1)S(1)}, bf16[1280,3,320]{0,2,1:T(8,128)(2,1)}, u32[]{:S(2)}) copy-start(bf16[1280,3,320]{0,2,1:T(8,128)(2,1)} %param.19) | copy-start | bytes 7372804
  8.0 4.1 %copy-start.5 = (bf16[1280]{0:T(1024)(128)(2,1)S(1)}, bf16[1280]{0:T(1024)(128)(2,1)}, u32[]{:S(2)}) copy-start(bf16[1280]{0:T(1024)(128)(2,1)} %param.21) | copy-start | bytes 7684
  8.0 97.8 %reduce-scatter.2.cloned.1.call-start = ((), (), s32[]{:S(2)}) async-start(), calls=%async_computation.6 | async-start | bytes 3276800 | tf_op jit(solution)/shard_map/reduce_scatter | solution.py:123
  8.1 3.3 %copy-start.1 = (bf16[512,1280]{1,0:T(8,128)(2,1)S(1)}, bf16[512,1280]{1,0:T(8,128)(2,1)}, u32[]{:S(2)}) copy-start(bf16[512,1280]{1,0:T(8,128)(2,1)} %param.16) | copy-start | bytes 3932164
  14.8 4.1 %copy-start.9 = (s32[2]{0:T(128)S(1)}, s32[2]{0:T(128)}, u32[]{:S(2)}) copy-start(s32[2]{0:T(128)} %param.17) | copy-start | bytes 28
  18.9 3.4 %copy-start.3 = (bf16[2,256,1,4,80]{1,0,4,3,2:T(2,128)(2,1)S(1)}, bf16[2,256,1,4,80]{1,0,4,3,2:T(2,128)(2,1)}, u32[]{:S(2)}) copy-start(bf16[2,256,1,4,80]{1,0,4,3,2:T(2,128)(2,1)} %get-tuple-element.16) | copy-start | bytes 983044
  24.9 3.7 %copy-start.12 = (bf16[80]{0:T(256)(128)(2,1)S(1)}, bf16[80]{0:T(256)(128)(2,1)}, u32[]{:S(2)}) copy-start(bf16[80]{0:T(256)(128)(2,1)} %param.24) | copy-start | bytes 484
  25.0 3.8 %copy-start.2 = (bf16[80,2048]{1,0:T(8,128)(2,1)S(1)}, bf16[80,2048]{1,0:T(8,128)(2,1)}, u32[]{:S(2)}) copy-start(bf16[80,2048]{1,0:T(8,128)(2,1)} %param.25) | copy-start | bytes 983044
  28.6 0.9 copy-start.4
  28.6 5.3 %copy-start.6 = (bf16[1280]{0:T(1024)(128)(2,1)S(1)}, bf16[1280]{0:T(1024)(128)(2,1)}, u32[]{:S(2)}) copy-start(bf16[1280]{0:T(1024)(128)(2,1)} %param.22) | copy-start | bytes 7684
  28.6 101.5 %all-gather.2.cloned.1.call-start = ((), (), s32[]{:S(2)}) async-start(), calls=%async_computation.7 | async-start | bytes 9400320 | tf_op jit(solution)/shard_map/all_gather | solution.py:16
  30.4 179.2 %all-reduce.2.cloned.1.call-start = ((), (), s32[]{:S(2)}) async-start(), calls=%async_computation.8 | async-start | bytes 2621440 | tf_op jit(solution)/shard_map/psum | solution.py:134
  221.9 8.6 %copy-start.7 = (bf16[2048]{0:T(1024)(128)(2,1)S(1)}, bf16[2048]{0:T(1024)(128)(2,1)}, u32[]{:S(2)}) copy-start(bf16[2048]{0:T(1024)(128)(2,1)} %param.26) | copy-start | bytes 12292
  221.9 8.6 %copy-start.10 = (s32[128]{0:T(128)S(1)}, s32[128]{0:T(128)}, u32[]{:S(2)}) copy-start(s32[128]{0:T(128)} %param.18) | copy-start | bytes 1540
  221.9 8.6 %copy-start.11 = (pred[128]{0:T(512)(128)(4,1)S(1)}, pred[128]{0:T(512)(128)(4,1)}, u32[]{:S(2)}) copy-start(pred[128]{0:T(512)(128)(4,1)} %constant.225) | copy-start | bytes 388
  221.9 30.5 %all-to-all-start.2 = ((bf16[4,128,2048]{2,1,0:T(8,128)(2,1)}), bf16[4,128,2048]{2,1,0:T(8,128)(2,1)}, u32[]{:S(2)}, u32[]{:S(2)}) async-start(bf16[4,128,2048]{2,1,0:T(8,128)(2,1)} %bitcast.61), calls=%async_computation.3 | async-start | bytes 4194304 | tf_op jit(solution)/shard_map/all_to_all | solution.py:48
  227.1 71.9 %collective-permute-start = (bf16[512,2048]{1,0:T(8,128)(2,1)}, bf16[512,2048]{1,0:T(8,128)(2,1)}, u32[]{:S(2)}, u32[]{:S(2)}) collective-permute-start(bf16[512,2048]{1,0:T(8,128)(2,1)} %param.28), channel_id=1, source_target_pairs={{0,16},{16,32},{32,48},{48,64},{64,80},{80,96},{96,112},{112,128},... | collective-permute-start | bytes 6291464 | tf_op jit(solution)/shard_map/ppermute | solution.py:55
  252.4 21.2 %all-to-all-start = ((s32[64,1,2]{2,1,0:T(1,128)}), s32[64,1,2]{2,1,0:T(1,128)S(1)}, u32[]{:S(2)}, u32[]{:S(2)}) async-start(s32[64,1,2]{2,1,0:T(1,128)} %bitcast.15), calls=%async_computation | async-start | bytes 65536 | tf_op jit(solution)/shard_map/all_to_all | solution.py:162
  273.6 20.5 %all-to-all-start.3 = ((bf16[64,2,2048]{2,1,0:T(2,128)(2,1)}), bf16[64,2,2048]{2,1,0:T(2,128)(2,1)S(1)}, u32[]{:S(2)}, u32[]{:S(2)}) async-start(bf16[64,2,2048]{2,1,0:T(2,128)(2,1)} %scatter_fusion), calls=%async_computation.4 | async-start | bytes 1048576 | tf_op jit(solution)/shard_map/all_to_all | solution.py:161
  298.9 6.8 %copy-start.8 = (bf16[2048]{0:T(1024)(128)(2,1)S(1)}, bf16[2048]{0:T(1024)(128)(2,1)}, u32[]{:S(2)}) copy-start(bf16[2048]{0:T(1024)(128)(2,1)} %param.29) | copy-start | bytes 12292
  301.9 11.6 %all-to-all-start.4 = ((f32[4,1,512]{2,1,0:T(1,128)}), f32[4,1,512]{2,1,0:T(1,128)S(1)}, u32[]{:S(2)}, u32[]{:S(2)}) async-start(f32[4,1,512]{2,1,0:T(1,128)} %broadcast_in_dim.31), calls=%async_computation.5 | async-start | bytes 16384 | tf_op jit(solution)/shard_map/all_to_all | solution.py:34
Sparse Core Ops, SparseCore 0:
  28.7 77.1 reduce-scatter.1
  135.5 73.9 all-reduce.1
Sparse Core Ops, SparseCore 1:
  30.9 99.1 all-gather.1
where the time goes:
time: 326 us; the launch traced here: 325 us
  waiting for transfers between devices  183 us (56%)
  local copies, waits for them, and re-layouts  33.5 us (10%)
  matrix products  29 us (9%)
  starting transfers between devices  27.7 us (8%)
  blocking collectives  19 us (6%)
  other arithmetic  16.8 us (5%)
  between operations  15.7 us (5%)
    psum x1, waiting for transfers between devices, per_device(): lax.psum(first_partial.astype(jnp.bfloat16), 'mp').astype(jnp.float32)  73 us
    reduce_scatter x1, waiting for transfers between devices, per_device(): lax.psum_scatter(partial_proj.reshape(merged_rows, 4, width), 'mp', scatt...  69.9 us
    all_to_all x1, blocking collectives, copy_for_each(): return lax.all_to_all(copies, axis, split_axis=0, concat_axis=0, tiled=True)  19 us
    all_to_all x1, waiting for transfers between devices, sent_and_summed(): lax.all_to_all(cut_along(value, dim, devices), axis, 0, 0, tiled=True)  18.9 us
    dot_general x1, matrix products, per_device(): jnp.dot(hidden, second_full, preferred_element_type=jnp.float32)  12.3 us
    all_to_all x1, waiting for transfers between devices, per_device(): lax.all_to_all(send_rows, ('section', 'dp'), split_axis=0, concat_axis=0,...  10.3 us
    all_to_all x1, starting transfers between devices, per_device(): lax.all_to_all(send_rows, ('section', 'dp'), split_axis=0, concat_axis=0,...  8.83 us
    scatter x1, local copies, waits for them, and re-layouts, per_device(): send_rows = jnp.zeros((group_count, run_cap, feature_cols), jnp.bfloat16)...  7.99 us
  transfers between devices with their start and end apart: 8, of which 6 were waited for; matrix products, arithmetic and copies ran while one was open for 10% of the time, Pallas kernels for 0%

commit v1 on v0

--- a/solution.py
+++ b/solution.py
@@ -2,6 +2,7 @@
 import jax.numpy as jnp
 from jax import lax
 from jax.sharding import PartitionSpec as P
+from jax.lax import all_gather
 
 HEAD_DIM = 80
 HID = 8192
@@ -131,7 +132,12 @@
     first_partial = jnp.dot(
         gathered_copies(merge_part, "dp", 0), first_full, preferred_element_type=jnp.float32
     )
-    first_total = lax.psum(first_partial.astype(jnp.bfloat16), "mp").astype(jnp.float32)
+
+    def carry_zone(t0, mesh_ax):
+        built = jnp.sum(all_gather(t0, mesh_ax), axis=0)
+        return built
+
+    first_total = carry_zone(first_partial.astype(jnp.bfloat16), mesh_ax="mp").astype(jnp.float32)
     hidden = jax.nn.gelu(first_total + bias_full.astype(jnp.float32), approximate=False).astype(
         jnp.bfloat16
     )

time: 326 us -> 361 us (1.11)
  waiting for transfers between devices: 183 us -> 202 us
  starting transfers between devices: 27.7 us -> 39 us
  other arithmetic: 16.8 us -> 21.5 us
    all_gather x0 -> x1, waiting for transfers between devices: none -> 92 us  [carry_zone(): built = jnp.sum(all_gather(t0, mesh_ax), axis=0)]
    psum x1 -> x0, waiting for transfers between devices: 73 us -> none  [per_device(): lax.psum(first_partial.astype(jnp.bfloat16), 'mp').astype(jnp.float32)]
    all_to_all x1, starting transfers between devices: 6.87 us -> 19 us  [per_device(): lax.all_to_all(send_place, ('section', 'dp'), split_axis=0, concat_axis=0...]
    reduce_sum x0 -> x1, other arithmetic: none -> 4.69 us  [carry_zone(): built = jnp.sum(all_gather(t0, mesh_ax), axis=0)]
  transfers between devices with their start and end apart: 8 -> 8, of which waited for: 6 -> 6; matrix products, arithmetic and copies ran while one was open for 10% -> 9% of each run, Pallas kernels for 0% -> 0%
where the time goes in v1:
time: 361 us; the launch traced here: 360 us
  waiting for transfers between devices  202 us (56%)
  starting transfers between devices  39 us (11%)
  local copies, waits for them, and re-layouts  33.5 us (9%)
  matrix products  29 us (8%)
  other arithmetic  21.5 us (6%)
  blocking collectives  19 us (5%)
  between operations  15.8 us (4%)
    all_gather x1, waiting for transfers between devices, carry_zone(): built = jnp.sum(all_gather(t0, mesh_ax), axis=0)  92 us
    reduce_scatter x1, waiting for transfers between devices, per_device(): lax.psum_scatter(partial_proj.reshape(merged_rows, 4, width), 'mp', scatt...  69.9 us
    all_to_all x1, blocking collectives, copy_for_each(): return lax.all_to_all(copies, axis, split_axis=0, concat_axis=0, tiled=True)  19 us
    all_to_all x1, starting transfers between devices, per_device(): lax.all_to_all(send_place, ('section', 'dp'), split_axis=0, concat_axis=0...  19 us
    all_to_all x1, waiting for transfers between devices, sent_and_summed(): lax.all_to_all(cut_along(value, dim, devices), axis, 0, 0, tiled=True)  18.9 us
    dot_general x1, matrix products, per_device(): jnp.dot(hidden, second_full, preferred_element_type=jnp.float32)  12.3 us
    all_to_all x1, waiting for transfers between devices, per_device(): lax.all_to_all(send_rows, ('section', 'dp'), split_axis=0, concat_axis=0,...  10.3 us
    all_to_all x1, starting transfers between devices, per_device(): lax.all_to_all(send_rows, ('section', 'dp'), split_axis=0, concat_axis=0,...  8.83 us
  transfers between devices with their start and end apart: 8, of which 6 were waited for; matrix products, arithmetic and copies ran while one was open for 9% of the time, Pallas kernels for 0%

profile of v1, /device:TPU:2, one launch (start us, length us, event | category | flops | bytes accessed | tf_op | source)
XLA Modules:
  0.0 360.0 jit_solution(5437647798026712291)
XLA Ops:
  8.0 0.0 copy-start
  8.0 0.0 reduce-scatter.2.cloned.1.call-start
  8.1 3.3 copy.100
  11.4 0.2 convert_reduce_fusion.1
  11.7 0.5 fusion.16
  12.2 2.6 convolution_convert_fusion
  14.8 2.5 reshape.190
  17.3 1.6 fusion.120
  18.9 0.1 iota_compare_fusion
  18.9 3.3 fusion.122
  22.2 1.9 fusion.69
  24.1 0.3 copy.59
  24.4 0.5 dot_general.23
  24.9 0.0 copy-start.12
  25.0 3.6 %fusion.73 = f32[128,4,1280]{2,0,1:T(8,128)} fusion(bf16[320,1280]{1,0:T(8,128)(2,1)} %param.20, bf16[128,4,320]{2,1,0:T(4,128)(2,1)S(1)} %dot_general.23), kind=kOutput, calls=%fused_computation.91 | convolution fusion | flops 419430400 | bytes 3768320 | tf_op jit(solution)/shard_map/dot_general | solution.py:119
  28.6 0.0 reduce-scatter.2.cloned.1.call-update
  28.6 0.0 all-gather.4.cloned.1.call-start
  28.7 0.1 copy.61
  28.8 0.7 copy-done.4
  29.5 0.8 pad_maximum_fusion
  30.3 0.0 all-gather.4.cloned.1.call-update
  30.4 0.0 all-gather.6.cloned.1.call-start
  30.4 3.5 reshape.188
  33.9 2.0 constant_dynamic-slice_fusion
  35.9 69.9 %reduce-scatter.2.cloned.1.call-done = f32[128,1,1280]{2,0,1:T(8,128)} async-done(((f32[128,4,1280]{2,0,1:T(8,128)}), f32[128,1,1280]{2,0,1:T(8,128)}) %reduce-scatter.2.cloned.1.call-update) | async-done | bytes 655376 | tf_op jit(solution)/shard_map/reduce_scatter | solution.py:124
  105.9 1.3 convert_reduce_fusion.2
  107.1 0.2 fusion.78
  107.4 0.2 fusion.80
  107.6 0.1 broadcast_in_dim.30
  107.7 19.0 %all_to_all.30 = bf16[4,128,1280]{2,1,0:T(8,128)(2,1)} all-to-all(bf16[4,128,1280]{2,1,0:T(8,128)(2,1)S(1)} %broadcast_in_dim.30), channel_id=1, replica_groups=mesh['section'=16,'dp'=4,'mp'=4] {'dp'}, dimensions={0} | all-to-all | bytes 2621440 | tf_op jit(solution)/shard_map/all_to_all | solution.py:35
  126.7 3.4 all-gather.4.cloned.1.call-done
  130.1 5.3 %fusion.10 = bf16[512,1280]{1,0:T(8,128)(2,1)} fusion(bf16[512,1280]{1,0:T(8,128)(2,1)} %bitcast.64, bf16[1280,3329]{1,0:T(8,128)(2,1)} %all-gather.4.cloned.1.call-done), kind=kOutput, calls=%fused_computation.19 | convolution fusion | flops 1678376960 | bytes 5898240 | tf_op jit(solution)/shard_map/dot_general | solution.py:132
  135.4 0.0 all-gather.6.cloned.1.call-update
  135.4 1.2 convert_reduce_fusion.3
  136.6 92.0 %all-gather.6.cloned.1.call-done = bf16[2048,1280]{1,0:T(8,128)(2,1)} async-done(((bf16[512,1280]{1,0:T(8,128)(2,1)}), bf16[2048,1280]{1,0:T(8,128)(2,1)}) %all-gather.6.cloned.1.call-update) | async-done | bytes 5242896 | tf_op jit(solution)/shard_map/all_gather | solution.py:137
  228.6 4.7 %reduce_sum.91 = bf16[512,1280]{1,0:T(8,128)(2,1)} reduce(bf16[4,512,1280]{2,1,0:T(8,128)(2,1)} %bitcast.62, bf16[]{:T(256)} %constant.179.clone.1), dimensions={0}, to_apply=%region_8.9 | reduce | flops 1966080 | bytes 6553602 | tf_op jit(solution)/shard_map/reduce_sum | solution.py:137
  233.3 12.3 %fusion.13 = bf16[512,2048]{1,0:T(8,128)(2,1)} fusion(bf16[1280,3329]{1,0:T(8,128)(2,1)} %all-gather.4.cloned.1.call-done, bf16[512,1280]{1,0:T(8,128)(2,1)} %reduce_sum.91, f32[1280]{0:T(1024)S(1)} %convert_reduce_fusion.3), kind=kOutput, calls=%fused_computation.20 | convolution fusion | flops 2729312256 | bytes 8655872 | tf_op jit(solution)/shard_map/dot_general | solution.py:145
  245.6 5.2 %all-to-all-start.2 = ((bf16[4,128,2048]{2,1,0:T(8,128)(2,1)}), bf16[4,128,2048]{2,1,0:T(8,128)(2,1)}, u32[]{:S(2)}, u32[]{:S(2)}) async-start(bf16[4,128,2048]{2,1,0:T(8,128)(2,1)} %bitcast.63), calls=%async_computation.3 | async-start | bytes 4194304 | tf_op jit(solution)/shard_map/all_to_all | solution.py:49
  250.8 2.6 collective-permute-start
  253.5 0.6 fusion.121
  254.1 1.2 compare_select_fusion.2
  255.3 0.1 reshape.185
  255.5 0.1 reshape.209
  255.6 0.1 fusion.83
  255.7 1.3 scatter_custom_fusion
  257.0 18.9 %all-to-all-done.2 = bf16[4,128,2048]{2,1,0:T(8,128)(2,1)} async-done(((bf16[4,128,2048]{2,1,0:T(8,128)(2,1)}), bf16[4,128,2048]{2,1,0:T(8,128)(2,1)}, u32[]{:S(2)}, u32[]{:S(2)}) %all-to-all-start.2) | async-done | bytes 2097184 | tf_op jit(solution)/shard_map/all_to_all | solution.py:49
  275.9 19.0 %all-to-all-start = ((s32[64,1,2]{2,1,0:T(1,128)}), s32[64,1,2]{2,1,0:T(1,128)S(1)}, u32[]{:S(2)}, u32[]{:S(2)}) async-start(s32[64,1,2]{2,1,0:T(1,128)} %bitcast.16), calls=%async_computation | async-start | bytes 65536 | tf_op jit(solution)/shard_map/all_to_all | solution.py:168
  294.8 2.1 convert_reduce_fusion
  296.9 1.6 reduce_sum.93
  298.5 1.6 add_convert_fusion
  300.1 1.1 broadcast_in_dim.24
  301.2 8.0 %scatter_fusion = bf16[64,2,2048]{2,1,0:T(2,128)(2,1)} fusion(bf16[64,2,2048]{2,1,0:T(2,128)(2,1)} %broadcast_in_dim.24, s32[64]{0:T(128)S(1)} %fusion.83, bf16[64,2,2048]{2,1,0:T(2,128)(2,1)S(1)} %add_convert_fusion), kind=kCustom, calls=%fused_computation.1 | custom fusion | bytes 1573120 | tf_op jit(solution)/shard_map/scatter | solution.py:159
  309.2 8.8 %all-to-all-start.3 = ((bf16[64,2,2048]{2,1,0:T(2,128)(2,1)}), bf16[64,2,2048]{2,1,0:T(2,128)(2,1)S(1)}, u32[]{:S(2)}, u32[]{:S(2)}) async-start(bf16[64,2,2048]{2,1,0:T(2,128)(2,1)} %scatter_fusion), calls=%async_computation.4 | async-start | bytes 1048576 | tf_op jit(solution)/shard_map/all_to_all | solution.py:167
  318.0 0.5 broadcast.203
  318.6 0.7 reduce.12
  319.3 0.1 reshape.187
  319.4 10.3 %all-to-all-done.3 = bf16[64,2,2048]{2,1,0:T(2,128)(2,1)S(1)} async-done(((bf16[64,2,2048]{2,1,0:T(2,128)(2,1)}), bf16[64,2,2048]{2,1,0:T(2,128)(2,1)S(1)}, u32[]{:S(2)}, u32[]{:S(2)}) %all-to-all-start.3) | async-done | bytes 524320 | tf_op jit(solution)/shard_map/all_to_all | solution.py:167
  329.7 0.2 reshape.225
  329.9 4.6 %scatter_fusion.1 = bf16[512,2048]{1,0:T(8,128)(2,1)} fusion(bf16[512,2048]{1,0:T(8,128)(2,1)} %copy.100, s32[128]{0:T(128)S(1)} %fusion.87, bf16[128,2048]{1,0:T(8,128)(2,1)S(1)} %reshape.225), kind=kCustom, calls=%fused_computation.2 | custom fusion | bytes 1573376 | tf_op jit(solution)/shard_map/scatter | solution.py:170
  334.5 2.4 fusion.3
  336.8 0.6 broadcast_in_dim.31
  337.5 3.2 all-to-all-start.4
  340.7 7.7 %all-to-all-done.4 = f32[4,1,512]{2,1,0:T(1,128)S(1)} async-done(((f32[4,1,512]{2,1,0:T(1,128)}), f32[4,1,512]{2,1,0:T(1,128)S(1)}, u32[]{:S(2)}, u32[]{:S(2)}) %all-to-all-start.4) | async-done | bytes 8224 | tf_op jit(solution)/shard_map/all_to_all | solution.py:35
  348.4 4.1 %fusion.5 = bf16[512,2048]{1,0:T(8,128)(2,1)} fusion(f32[2048]{0:T(1024)S(1)} %convert_element_type.107, f32[512]{0:T(512)S(1)} %add_rsqrt_fusion, bf16[512,2048]{1,0:T(8,128)(2,1)} %scatter_fusion.1, bf16[512,2048]{1,0:T(8,128)(2,1)} %collective-permute-done, pred[]{:T(512)S(6)} %eq.6), kind=kLoop, calls=%fused_computation.10 | loop fusion | flops 5242880 | bytes 6301697 | tf_op jit(solution)/shard_map/convert_element_type | solution.py:180
  (36 shorter events, 0.1 us)
Async XLA Ops:
  8.0 4.2 %copy-start = (bf16[1280,3,320]{0,2,1:T(8,128)(2,1)S(1)}, bf16[1280,3,320]{0,2,1:T(8,128)(2,1)}, u32[]{:S(2)}) copy-start(bf16[1280,3,320]{0,2,1:T(8,128)(2,1)} %param.19) | copy-start | bytes 7372804
  8.0 4.1 %copy-start.5 = (bf16[1280]{0:T(1024)(128)(2,1)S(1)}, bf16[1280]{0:T(1024)(128)(2,1)}, u32[]{:S(2)}) copy-start(bf16[1280]{0:T(1024)(128)(2,1)} %param.21) | copy-start | bytes 7684
  8.0 97.8 %reduce-scatter.2.cloned.1.call-start = ((), (), s32[]{:S(2)}) async-start(), calls=%async_computation.6 | async-start | bytes 3276800 | tf_op jit(solution)/shard_map/reduce_scatter | solution.py:124
  8.1 3.3 copy-start.1
  14.8 4.1 %copy-start.9 = (s32[2]{0:T(128)S(1)}, s32[2]{0:T(128)}, u32[]{:S(2)}) copy-start(s32[2]{0:T(128)} %param.17) | copy-start | bytes 28
  18.9 3.4 copy-start.3
  24.9 3.7 %copy-start.12 = (bf16[80]{0:T(256)(128)(2,1)S(1)}, bf16[80]{0:T(256)(128)(2,1)}, u32[]{:S(2)}) copy-start(bf16[80]{0:T(256)(128)(2,1)} %param.24) | copy-start | bytes 484
  25.0 3.8 %copy-start.2 = (bf16[80,2048]{1,0:T(8,128)(2,1)S(1)}, bf16[80,2048]{1,0:T(8,128)(2,1)}, u32[]{:S(2)}) copy-start(bf16[80,2048]{1,0:T(8,128)(2,1)} %param.25) | copy-start | bytes 983044
  28.6 0.9 copy-start.4
  28.6 5.3 %copy-start.6 = (bf16[1280]{0:T(1024)(128)(2,1)S(1)}, bf16[1280]{0:T(1024)(128)(2,1)}, u32[]{:S(2)}) copy-start(bf16[1280]{0:T(1024)(128)(2,1)} %param.22) | copy-start | bytes 7684
  28.6 101.5 %all-gather.4.cloned.1.call-start = ((), (), s32[]{:S(2)}) async-start(), calls=%async_computation.7 | async-start | bytes 9400320 | tf_op jit(solution)/shard_map/all_gather | solution.py:17
  30.4 198.2 %all-gather.6.cloned.1.call-start = ((), (), s32[]{:S(2)}) async-start(), calls=%async_computation.8 | async-start | bytes 6553600 | tf_op jit(solution)/shard_map/all_gather | solution.py:137
  245.6 8.4 %copy-start.7 = (bf16[2048]{0:T(1024)(128)(2,1)S(1)}, bf16[2048]{0:T(1024)(128)(2,1)}, u32[]{:S(2)}) copy-start(bf16[2048]{0:T(1024)(128)(2,1)} %param.26) | copy-start | bytes 12292
  245.6 8.4 %copy-start.10 = (s32[128]{0:T(128)S(1)}, s32[128]{0:T(128)}, u32[]{:S(2)}) copy-start(s32[128]{0:T(128)} %param.18) | copy-start | bytes 1540
  245.6 8.4 %copy-start.11 = (pred[128]{0:T(512)(128)(4,1)S(1)}, pred[128]{0:T(512)(128)(4,1)}, u32[]{:S(2)}) copy-start(pred[128]{0:T(512)(128)(4,1)} %constant.226) | copy-start | bytes 388
  245.6 30.2 %all-to-all-start.2 = ((bf16[4,128,2048]{2,1,0:T(8,128)(2,1)}), bf16[4,128,2048]{2,1,0:T(8,128)(2,1)}, u32[]{:S(2)}, u32[]{:S(2)}) async-start(bf16[4,128,2048]{2,1,0:T(8,128)(2,1)} %bitcast.63), calls=%async_computation.3 | async-start | bytes 4194304 | tf_op jit(solution)/shard_map/all_to_all | solution.py:49
  250.8 83.7 %collective-permute-start = (bf16[512,2048]{1,0:T(8,128)(2,1)}, bf16[512,2048]{1,0:T(8,128)(2,1)}, u32[]{:S(2)}, u32[]{:S(2)}) collective-permute-start(bf16[512,2048]{1,0:T(8,128)(2,1)} %param.28), channel_id=1, source_target_pairs={{0,16},{16,32},{32,48},{48,64},{64,80},{80,96},{96,112},{112,128},... | collective-permute-start | bytes 6291464 | tf_op jit(solution)/shard_map/ppermute | solution.py:56
  275.9 33.3 %all-to-all-start = ((s32[64,1,2]{2,1,0:T(1,128)}), s32[64,1,2]{2,1,0:T(1,128)S(1)}, u32[]{:S(2)}, u32[]{:S(2)}) async-start(s32[64,1,2]{2,1,0:T(1,128)} %bitcast.16), calls=%async_computation | async-start | bytes 65536 | tf_op jit(solution)/shard_map/all_to_all | solution.py:168
  309.2 20.5 %all-to-all-start.3 = ((bf16[64,2,2048]{2,1,0:T(2,128)(2,1)}), bf16[64,2,2048]{2,1,0:T(2,128)(2,1)S(1)}, u32[]{:S(2)}, u32[]{:S(2)}) async-start(bf16[64,2,2048]{2,1,0:T(2,128)(2,1)} %scatter_fusion), calls=%async_computation.4 | async-start | bytes 1048576 | tf_op jit(solution)/shard_map/all_to_all | solution.py:167
  334.5 6.2 %copy-start.8 = (bf16[2048]{0:T(1024)(128)(2,1)S(1)}, bf16[2048]{0:T(1024)(128)(2,1)}, u32[]{:S(2)}) copy-start(bf16[2048]{0:T(1024)(128)(2,1)} %param.29) | copy-start | bytes 12292
  337.5 11.0 %all-to-all-start.4 = ((f32[4,1,512]{2,1,0:T(1,128)}), f32[4,1,512]{2,1,0:T(1,128)S(1)}, u32[]{:S(2)}, u32[]{:S(2)}) async-start(f32[4,1,512]{2,1,0:T(1,128)} %broadcast_in_dim.31), calls=%async_computation.5 | async-start | bytes 16384 | tf_op jit(solution)/shard_map/all_to_all | solution.py:35
Sparse Core Ops, SparseCore 0:
  28.7 77.1 reduce-scatter.1
  135.5 92.9 all-gather.5
Sparse Core Ops, SparseCore 1:
  30.9 99.1 all-gather.3
